TPU v7x, 32 devices: a whole 2x2x4 slice. The times are simulated.
32 devices in a mesh: tile: 16 (over z, y, x), lev: 2 (over core).
Axes of the slice: x: 2, y: 2, z: 4, core: 2. Of those that a mesh axis runs over, the one named last changes fastest.
Arguments:
- increments: bfloat16 [136, 256, 1024], P('lev', 'tile'), may hold values from -30 to 30
- projection: bfloat16 [80, 136], replicated, may hold values from -0.5 to 0.5
- helmholtz: float32 [80], P('lev'), may hold values from 0.05 to 4
Outputs:
- solution: float32 [80, 256, 1024], P('lev', 'tile')
- residual: float32 [80, 256, 1024], P('lev', 'tile')
All inputs are finite; a program needn't handle non-finite values.
Results may differ from a plain program's by a relative error of at most 0.00075.
Values may be sent and summed in bfloat16 or wider, within the bound.
A program may use at most 192 MiB of HBM per device.

v0:
```python
import jax
import jax.numpy as jnp
import numpy as np
from jax import lax
from jax.sharding import PartitionSpec as P

S = 4
BLOCKS = 2
highest = lax.Precision.HIGHEST


def extended(block, sides, width):
    for axis, dim in sides:
        count = lax.axis_size(axis)
        forward = [(i, i + 1) for i in range(count - 1)]
        backward = [(target, source) for source, target in forward]
        low = lax.ppermute(
            lax.slice_in_dim(block, block.shape[dim] - width, None, axis=dim), axis, forward
        )
        high = lax.ppermute(lax.slice_in_dim(block, 0, width, axis=dim), axis, backward)
        block = jnp.concatenate([low, block, high], axis=dim)
    return block


def shift_matrix():
    width = 2 * S + 1
    table = np.zeros((width, width), np.float32)
    for index in range(S):
        table[index + 1, index] = 1.0
    for index in range(S - 1):
        table[S + 2 + index, S + 1 + index] = 1.0
    return jnp.asarray(table, jnp.float32)


def stencil_rows(field, weight_col):
    padded = extended(field, (("tile", 1),), 1)
    side = jnp.pad(field, ((0, 0), (0, 0), (1, 1)))
    beside_all = padded[:, 2:, :] + padded[:, :-2, :] + side[:, :, 2:] + side[:, :, :-2]
    return weight_col * beside_all


def quadratic(gram, left, right):
    return jnp.einsum("ma,mab,mb->m", left, gram, right, precision=highest)


def combine(coef, vectors):
    total = coef[:, 0, None, None] * vectors[0]
    for index in range(1, len(vectors)):
        total = total + coef[:, index, None, None] * vectors[index]
    return total


def inner_table(vectors):
    width = len(vectors)
    cached = {}
    for first in range(width):
        for second in range(first, width):
            cached[first, second] = jnp.sum(vectors[first] * vectors[second], axis=(1, 2))
    rows_list = []
    for first in range(width):
        entries = []
        for second in range(width):
            entries.append(cached[min(first, second), max(first, second)])
        rows_list.append(jnp.stack(entries, axis=1))
    return jnp.stack(rows_list, axis=1)


def shards(increments, projection, helmholtz):
    lev_count, rows_x, cells_y = increments.shape
    mode_count = projection.shape[0] // lax.axis_size("lev")
    flat = increments.reshape(lev_count, rows_x * cells_y)
    own_cols = lax.dynamic_slice_in_dim(projection, lax.axis_index("lev") * lev_count, lev_count, 1)
    modal = lax.psum_scatter(
        jnp.dot(own_cols, flat, preferred_element_type=jnp.float32),
        "lev",
        scatter_dimension=0,
        tiled=True,
    )
    modal = modal.reshape(mode_count, rows_x, cells_y)
    weight_col = (1.0 / (4.0 + helmholtz))[:, None, None]
    width = 2 * S + 1
    shifter = shift_matrix()
    solution = jnp.zeros_like(modal)
    resid = modal
    direction = modal
    for block_index in range(BLOCKS):
        vectors = [direction]
        current = direction
        for power_index in range(S):
            current = stencil_rows(current, weight_col)
            vectors.append(current)
        vectors.append(resid)
        current = resid
        for power_index in range(S - 1):
            current = stencil_rows(current, weight_col)
            vectors.append(current)
        gram = inner_table(vectors)
        gram = lax.psum(gram, "tile")
        p_coef = jnp.zeros((mode_count, width), jnp.float32).at[:, 0].set(1.0)
        r_coef = jnp.zeros((mode_count, width), jnp.float32).at[:, S + 1].set(1.0)
        x_coef = jnp.zeros((mode_count, width), jnp.float32)
        squares = quadratic(gram, r_coef, r_coef)
        for step_index in range(S):
            moved = p_coef - jnp.einsum("ab,mb->ma", shifter, p_coef, precision=highest)
            alpha = (squares / quadratic(gram, p_coef, moved))[:, None]
            x_coef = x_coef + alpha * p_coef
            r_coef = r_coef - alpha * moved
            fresh = quadratic(gram, r_coef, r_coef)
            p_coef = r_coef + (fresh / squares)[:, None] * p_coef
            squares = fresh
        solution = solution + combine(x_coef, vectors)
        resid = combine(r_coef, vectors)
        direction = combine(p_coef, vectors)
    return (solution, resid)


def solution(mesh):
    in_specs = (P("lev", "tile", None), P(), P("lev"))
    out_specs = (P("lev", "tile", None), P("lev", "tile", None))
    return jax.shard_map(shards, mesh=mesh, in_specs=in_specs, out_specs=out_specs, check_vma=False)
```

profile of v0, /device:TPU:0, one launch (start us, length us, event | category | flops | bytes accessed | tf_op | source)
XLA Modules:
  0.0 469.2 jit_solution(7739262353369601456)
XLA Ops:
  7.2 2.0 pad.144
  9.2 2.9 copy.235
  12.1 4.9 %fusion.44 = f32[80,16384]{1,0:T(8,128)} fusion(bf16[68,16384]{1,0:T(8,128)(2,1)} %bitcast.230, bf16[80,136]{0,1:T(8,128)(2,1)S(1)} %copy-done, s32[]{:T(128)S(6)} %select_n.3), kind=kOutput, calls=%fused_computation.212 | convolution fusion | flops 178257920 | bytes 7489540 | tf_op jit(solution)/shard_map/dot_general | solution.py:74
  17.0 15.9 %reduce-scatter.2.cloned.1.call-done = f32[40,16384]{1,0:T(8,128)} async-done(((f32[80,16384]{1,0:T(8,128)}), f32[40,16384]{1,0:T(8,128)}) %reduce-scatter.2.cloned.1.call-update) | async-done | bytes 2621456 | tf_op jit(solution)/shard_map/reduce_scatter | solution.py:73
  32.9 2.0 copy.251
  35.0 1.3 collective-permute-start
  36.3 4.6 collective-permute-start.1
  40.9 2.4 collective-permute-done
  43.3 4.5 collective-permute-done.1
  47.8 1.4 fusion.2
  52.1 5.0 %collective-permute-start.3 = (f32[40,1,1024]{2,0,1:T(8,128)S(1)}, f32[40,1,1024]{2,0,1:T(8,128)S(1)}, u32[]{:S(2)}, u32[]{:S(2)}) collective-permute-start(f32[40,1,1024]{2,0,1:T(8,128)S(1)} %get-tuple-element.129), channel_id=1, source_target_pairs={{0,2},{2,4},{4,6},{6,8},{8,10},{10,12},{12,14},{14,16},{16,18},{18... | collective-permute-start | bytes 491528 | tf_op jit(solution)/shard_map/ppermute | solution.py:17
  59.9 1.9 collective-permute-done.3
  61.8 5.6 %fusion.5 = f32[40,16,1024]{2,0,1:T(8,128)S(1)} fusion(f32[40,16,1024]{2,0,1:T(8,128)} %copy-done.18, f32[40,1,1024]{2,0,1:T(8,128)S(1)} %collective-permute-done.3, f32[40,1,1024]{2,0,1:T(8,128)S(1)} %collective-permute-done.2, f32[40]{0:T(128)S(1)} %add_divide_fusion), kind=kLoop, calls=%fused_computation.27 | loop fusion | flops 3932160 | bytes 5570720 | tf_op jit(solution)/shard_map/mul | solution.py:39
  69.6 5.0 %collective-permute-start.5 = (f32[40,1,1024]{2,0,1:T(8,128)}, f32[40,1,1024]{2,0,1:T(8,128)S(1)}, u32[]{:S(2)}, u32[]{:S(2)}) collective-permute-start(f32[40,1,1024]{2,0,1:T(8,128)} %get-tuple-element.127), channel_id=1, source_target_pairs={{0,2},{2,4},{4,6},{6,8},{8,10},{10,12},{12,14},{14,16},{16,18},{18... | collective-permute-start | bytes 491528 | tf_op jit(solution)/shard_map/ppermute | solution.py:17
  75.0 2.3 collective-permute-done.4
  77.3 4.5 collective-permute-done.5
  81.8 5.5 %fusion.8 = f32[40,16,1024]{2,0,1:T(8,128)S(1)} fusion(f32[40,16,1024]{2,0,1:T(8,128)} %copy-done.6, f32[40,1,1024]{2,0,1:T(8,128)S(1)} %collective-permute-done.5, f32[40,1,1024]{2,0,1:T(8,128)S(1)} %collective-permute-done.4, f32[40]{0:T(128)S(1)} %add_divide_fusion), kind=kLoop, calls=%fused_computation.30 | loop fusion | flops 3932160 | bytes 5570720 | tf_op jit(solution)/shard_map/mul | solution.py:39
  87.4 1.6 collective-permute-start.6
  88.9 4.9 %collective-permute-start.7 = (f32[40,1,1024]{2,0,1:T(8,128)S(1)}, f32[40,1,1024]{2,0,1:T(8,128)S(1)}, u32[]{:S(2)}, u32[]{:S(2)}) collective-permute-start(f32[40,1,1024]{2,0,1:T(8,128)S(1)} %get-tuple-element.125), channel_id=1, source_target_pairs={{0,2},{2,4},{4,6},{6,8},{8,10},{10,12},{12,14},{14,16},{16,18},{18... | collective-permute-start | bytes 491528 | tf_op jit(solution)/shard_map/ppermute | solution.py:17
  94.1 2.2 collective-permute-done.6
  96.3 2.2 collective-permute-done.7
  98.5 5.4 %multiply_reduce_fusion.45 = (f32[40]{0:T(128)S(1)}, f32[40]{0:T(128)S(1)}, f32[40]{0:T(128)S(1)}, f32[40]{0:T(128)S(1)}, f32[40]{0:T(128)S(1)}, /*index=5*/f32[...) fusion(f32[40,16,1024]{2,0,1:T(8,128)S(1)} %fusion.8, ...), kind=kLoop, calls=%fused_computation.138 | loop fusion | flops 26213840 | bytes 11143520 | tf_op jit(solution)/shard_map/reduce_sum | solution.py:58
  104.2 75.3 %psum.14 = f32[40,9,9]{0,2,1:T(8,128)S(1)} all-reduce(f32[40,9,9]{0,2,1:T(8,128)S(1)} %constant_dynamic-update-slice_fusion), channel_id=1, replica_groups=mesh['tile'=16,'lev'=2] {'tile'}, use_global_device_ids=true, to_apply=%region_17.18 | all-reduce | flops 3240 | bytes 25920 | tf_op jit(solution)/shard_map/psum | solution.py:98
  183.8 13.6 %multiply_add_fusion.2 = f32[40,16,1024]{2,0,1:T(8,128)S(1)} fusion(f32[40,16,1024]{2,0,1:T(8,128)} %copy-done.6, f32[40,16,1024]{2,0,1:T(8,128)} %get-tuple-element.109, f32[40]{0:T(128)S(1)} %get-tuple-element.162, f32[40]{0:T(128)S(1)} %get-tuple-element.163, f32[40]{0:T(128)S(1)} %get-tuple-element.164, f32[40]{0:T(128)S(1)} %get-tuple-element.165, ...), kind=kLoop, calls=%fused_computation.137 | loop fusion | flops 19005440 | bytes 13764160 | tf_op jit(solution)/shard_map/add | solution.py:49
  197.4 1.3 collective-permute-start.8
  198.7 4.6 collective-permute-start.9
  203.3 5.8 %multiply_add_fusion.1 = f32[40,16,1024]{2,0,1:T(8,128)S(1)} fusion(f32[40,16,1024]{2,0,1:T(8,128)S(1)} %copy-done.7, f32[40,16,1024]{2,0,1:T(8,128)S(1)} %copy-done.17, f32[40]{0:T(128)S(1)} %get-tuple-element.171, f32[40]{0:T(128)S(1)} %get-tuple-element.172, f32[40]{0:T(128)S(1)} %get-tuple-element.173, f32[40]{0:T(128)S(1)} %get-tuple-element.174, ...), kind=kLoop, calls=%fused_computation.131 | loop fusion | flops 19005440 | bytes 13764160 | tf_op jit(solution)/shard_map/add | solution.py:49
  209.2 1.4 fusion.14
  211.9 4.6 collective-permute-start.11
  217.8 4.6 collective-permute-start.17
  222.4 1.4 fusion.17
  225.2 5.0 %collective-permute-start.13 = (f32[40,1,1024]{2,0,1:T(8,128)S(1)}, f32[40,1,1024]{2,0,1:T(8,128)S(1)}, u32[]{:S(2)}, u32[]{:S(2)}) collective-permute-start(f32[40,1,1024]{2,0,1:T(8,128)S(1)} %get-tuple-element.115), channel_id=1, source_target_pairs={{0,2},{2,4},{4,6},{6,8},{8,10},{10,12},{12,14},{14,16},{16,18},{18... | collective-permute-start | bytes 491528 | tf_op jit(solution)/shard_map/ppermute | solution.py:17
  230.2 2.3 collective-permute-done.12
  232.6 2.0 collective-permute-done.13
  234.5 3.3 fusion.20
  239.2 6.9 %collective-permute-start.19 = (f32[40,1,1024]{2,0,1:T(8,128)S(1)}, f32[40,1,1024]{2,0,1:T(8,128)S(1)}, u32[]{:S(2)}, u32[]{:S(2)}) collective-permute-start(f32[40,1,1024]{2,0,1:T(8,128)S(1)} %get-tuple-element.121), channel_id=1, source_target_pairs={{0,2},{2,4},{4,6},{6,8},{8,10},{10,12},{12,14},{14,16},{16,18},{18... | collective-permute-start | bytes 491528 | tf_op jit(solution)/shard_map/ppermute | solution.py:17
  247.4 6.1 %collective-permute-start.15 = (f32[40,1,1024]{2,0,1:T(8,128)S(1)}, f32[40,1,1024]{2,0,1:T(8,128)}, u32[]{:S(2)}, u32[]{:S(2)}) collective-permute-start(f32[40,1,1024]{2,0,1:T(8,128)S(1)} %get-tuple-element.113), channel_id=1, source_target_pairs={{0,2},{2,4},{4,6},{6,8},{8,10},{10,12},{12,14},{14,16},{16,18},{18... | collective-permute-start | bytes 491528 | tf_op jit(solution)/shard_map/ppermute | solution.py:17
  253.6 1.4 fusion.29
  255.1 1.5 copy-done.20
  257.8 5.7 %collective-permute-start.21 = (f32[40,1,1024]{2,0,1:T(8,128)S(1)}, f32[40,1,1024]{2,0,1:T(8,128)}, u32[]{:S(2)}, u32[]{:S(2)}) collective-permute-start(f32[40,1,1024]{2,0,1:T(8,128)S(1)} %get-tuple-element.111), channel_id=1, source_target_pairs={{0,2},{2,4},{4,6},{6,8},{8,10},{10,12},{12,14},{14,16},{16,18},{18... | collective-permute-start | bytes 491528 | tf_op jit(solution)/shard_map/ppermute | solution.py:17
  264.3 1.4 collective-permute-done.21
  265.7 24.5 %multiply_reduce_fusion = (f32[40]{0:T(128)}, f32[40]{0:T(128)}, f32[40]{0:T(128)}, f32[40]{0:T(128)}, f32[40]{0:T(128)}, /*index=5*/f32[40]{0:T(128)}, f32[40]{...) fusion(f32[40,16,1024]{2,0,1:T(8,128)} %copy-done.20, ...), kind=kLoop, calls=%fused_computation.91 | loop fusion | flops 70777080 | bytes 21961920 | tf_op jit(solution)/shard_map/reduce_sum | solution.py:58
  290.4 1.4 stack.467
  291.8 1.4 stack.464
  293.2 1.4 stack.460
  294.5 1.4 stack.455
  295.9 1.4 stack.449
  297.3 1.4 stack.442
  298.7 1.3 stack.434
  300.1 1.3 stack.425
  301.4 1.4 stack.415
  308.2 77.3 %psum.15 = f32[40,9,9]{0,2,1:T(8,128)S(1)} all-reduce(f32[40,9,9]{0,2,1:T(8,128)} %constant_dynamic-update-slice_fusion.9), channel_id=1, replica_groups=mesh['tile'=16,'lev'=2] {'tile'}, use_global_device_ids=true, to_apply=%region_64.65 | all-reduce | flops 3240 | bytes 25920 | tf_op jit(solution)/shard_map/psum | solution.py:98
  385.5 1.4 multiply_reduce_fusion.66
  386.9 1.4 copy.117
  388.3 1.4 multiply_reduce_fusion.83
  393.7 1.4 copy.126
  399.5 1.4 copy.139
  408.7 1.4 copy.153
  410.1 1.4 copy.157
  414.2 1.4 copy.166
  422.2 19.2 %multiply_add_fusion = f32[40,16,1024]{2,0,1:T(8,128)} fusion(f32[40,16,1024]{2,0,1:T(8,128)} %get-tuple-element.108, f32[40,16,1024]{2,0,1:T(8,128)} %copy-done.15, f32[40,16,1024]{2,0,1:T(8,128)} %copy-done.11, f32[40,16,1024]{2,0,1:T(8,128)} %get-tuple-element.107, f32[40,16,1024]{2,0,1:T(8,128)} %copy-done.16, f32[40,16,1024]{2,0,1:T(8,128)} %copy-done.13, ...), kind=kLoop, calls=%fused_computation.89 | loop fusion | flops 19005440 | bytes 21628480 | tf_op jit(solution)/shard_map/add | solution.py:49
  441.5 4.9 %copy.22 = f32[40,16,1024]{2,1,0:T(8,128)} copy(f32[40,16,1024]{2,0,1:T(8,128)} %multiply_add_fusion) | data formatting | bytes 5242880
  446.5 12.8 %add_add_fusion = f32[40,16,1024]{2,0,1:T(8,128)S(1)} fusion(f32[40,16,1024]{2,0,1:T(8,128)} %get-tuple-element.108, f32[40,16,1024]{2,0,1:T(8,128)} %copy-done.15, f32[40,16,1024]{2,0,1:T(8,128)S(1)} %copy-done.12, f32[40,16,1024]{2,0,1:T(8,128)} %get-tuple-element.107, f32[40,16,1024]{2,0,1:T(8,128)} %copy-done.16, f32[40,16,1024]{2,0,1:T(8,128)S(1)} %copy-done.14, ...), kind=kLoop, calls=%fused_computation.90 | loop fusion | flops 38666240 | bytes 32771040 | tf_op jit(solution)/shard_map/add | solution.py:111
  459.3 3.0 copy.21
  (303 shorter events, 51.3 us)
Async XLA Ops:
  7.2 25.7 %reduce-scatter.2.cloned.1.call-start = ((), (), s32[]{:S(2)}) async-start(), calls=%async_computation.1 | async-start | bytes 7864320 | tf_op jit(solution)/shard_map/reduce_scatter | solution.py:73
  32.9 8.0 %copy-start.72 = (f32[40]{0:T(128)S(1)}, f32[40]{0:T(128)}, u32[]{:S(2)}) copy-start(f32[40]{0:T(128)} %param.14) | copy-start | bytes 484
  34.9 14.3 %copy-start.3 = (f32[5,16,8,1024]{3,2,0,1:T(8,128)}, f32[5,16,8,1024]{3,2,0,1:T(8,128)S(1)}, u32[]{:S(2)}) copy-start(f32[5,16,8,1024]{3,2,0,1:T(8,128)S(1)} %copy.251) | copy-start | bytes 7864324
  35.0 8.3 %collective-permute-start = (f32[40,1,1024]{2,0,1:T(8,128)S(1)}, f32[40,1,1024]{2,0,1:T(8,128)S(1)}, u32[]{:S(2)}, u32[]{:S(2)}) collective-permute-start(f32[40,1,1024]{2,0,1:T(8,128)S(1)} %get-tuple-element.130), channel_id=1, source_target_pairs={{2,0},{4,2},{6,4},{8,6},{10,8},{12,10},{14,12},{16,14},{18,16},{20... | collective-permute-start | bytes 491528 | tf_op jit(solution)/shard_map/ppermute | solution.py:20
  36.3 11.5 %collective-permute-start.1 = (f32[40,1,1024]{2,0,1:T(8,128)S(1)}, f32[40,1,1024]{2,0,1:T(8,128)S(1)}, u32[]{:S(2)}, u32[]{:S(2)}) collective-permute-start(f32[40,1,1024]{2,0,1:T(8,128)S(1)} %get-tuple-element.131), channel_id=1, source_target_pairs={{0,2},{2,4},{4,6},{6,8},{8,10},{10,12},{12,14},{14,16},{16,18},{18... | collective-permute-start | bytes 491528 | tf_op jit(solution)/shard_map/ppermute | solution.py:17
  40.9 142.9 %copy-start.35 = (f32[40]{0:T(128)}, f32[40]{0:T(128)S(1)}, u32[]{:S(2)}) copy-start(f32[40]{0:T(128)S(1)} %add_divide_fusion) | copy-start | bytes 484
  50.8 9.1 %collective-permute-start.2 = (f32[40,1,1024]{2,0,1:T(8,128)}, f32[40,1,1024]{2,0,1:T(8,128)S(1)}, u32[]{:S(2)}, u32[]{:S(2)}) collective-permute-start(f32[40,1,1024]{2,0,1:T(8,128)} %get-tuple-element.128), channel_id=1, source_target_pairs={{2,0},{4,2},{6,4},{8,6},{10,8},{12,10},{14,12},{16,14},{18,16},{20... | collective-permute-start | bytes 491528 | tf_op jit(solution)/shard_map/ppermute | solution.py:20
  52.1 9.7 %collective-permute-start.3 = (f32[40,1,1024]{2,0,1:T(8,128)S(1)}, f32[40,1,1024]{2,0,1:T(8,128)S(1)}, u32[]{:S(2)}, u32[]{:S(2)}) collective-permute-start(f32[40,1,1024]{2,0,1:T(8,128)S(1)} %get-tuple-element.129), channel_id=1, source_target_pairs={{0,2},{2,4},{4,6},{6,8},{8,10},{10,12},{12,14},{14,16},{16,18},{18... | collective-permute-start | bytes 491528 | tf_op jit(solution)/shard_map/ppermute | solution.py:17
  59.9 121.4 %copy-start.39 = (f32[9]{0:T(128)}, f32[9]{0:T(128)S(1)}, u32[]{:S(2)}) copy-start(f32[9]{0:T(128)S(1)} %scatter.16) | copy-start | bytes 112
  59.9 14.8 %copy-start.30 = (f32[9,9]{1,0:T(8,128)S(1)}, f32[9,9]{1,0:T(8,128)}, u32[]{:S(2)}) copy-start(f32[9,9]{1,0:T(8,128)} %constant.100.clone) | copy-start | bytes 976
  59.9 7.6 %copy-start.26 = (f32[40,1,1024]{2,0,1:T(8,128)}, f32[40,1,1024]{2,0,1:T(8,128)S(1)}, u32[]{:S(2)}) copy-start(f32[40,1,1024]{2,0,1:T(8,128)S(1)} %collective-permute-done.2) | copy-start | bytes 491524
  61.8 5.7 %copy-start.28 = (f32[40,1,1024]{2,0,1:T(8,128)}, f32[40,1,1024]{2,0,1:T(8,128)S(1)}, u32[]{:S(2)}) copy-start(f32[40,1,1024]{2,0,1:T(8,128)S(1)} %collective-permute-done.3) | copy-start | bytes 491524
  67.5 7.4 %copy-start.6 = (f32[40,16,1024]{2,0,1:T(8,128)}, f32[40,16,1024]{2,0,1:T(8,128)S(1)}, u32[]{:S(2)}) copy-start(f32[40,16,1024]{2,0,1:T(8,128)S(1)} %fusion.5) | copy-start | bytes 7864324
  68.3 9.0 %collective-permute-start.4 = (f32[40,1,1024]{2,0,1:T(8,128)}, f32[40,1,1024]{2,0,1:T(8,128)S(1)}, u32[]{:S(2)}, u32[]{:S(2)}) collective-permute-start(f32[40,1,1024]{2,0,1:T(8,128)} %get-tuple-element.126), channel_id=1, source_target_pairs={{2,0},{4,2},{6,4},{8,6},{10,8},{12,10},{14,12},{16,14},{18,16},{20... | collective-permute-start | bytes 491528 | tf_op jit(solution)/shard_map/ppermute | solution.py:20
  69.6 12.2 %collective-permute-start.5 = (f32[40,1,1024]{2,0,1:T(8,128)}, f32[40,1,1024]{2,0,1:T(8,128)S(1)}, u32[]{:S(2)}, u32[]{:S(2)}) collective-permute-start(f32[40,1,1024]{2,0,1:T(8,128)} %get-tuple-element.127), channel_id=1, source_target_pairs={{0,2},{2,4},{4,6},{6,8},{8,10},{10,12},{12,14},{14,16},{16,18},{18... | collective-permute-start | bytes 491528 | tf_op jit(solution)/shard_map/ppermute | solution.py:17
  74.9 108.1 %copy-start.24 = (f32[40,9]{0,1:T(8,128)}, f32[40,9]{0,1:T(8,128)S(1)}, u32[]{:S(2)}) copy-start(f32[40,9]{0,1:T(8,128)S(1)} %convolution_subtract_fusion.6) | copy-start | bytes 4324
  75.0 104.8 %copy-start.33 = (f32[40,9]{1,0:T(8,128)}, f32[40,9]{1,0:T(8,128)S(1)}, u32[]{:S(2)}) copy-start(f32[40,9]{1,0:T(8,128)S(1)} %copy.40) | copy-start | bytes 4324
  75.0 18.9 %copy-start.2 = (f32[40,16384]{1,0:T(8,128)S(1)}, f32[40,16384]{1,0:T(8,128)}, u32[]{:S(2)}) copy-start(f32[40,16384]{1,0:T(8,128)} %reduce-scatter.2.cloned.1.call-done) | copy-start | bytes 7864324
  81.8 121.4 %copy-start.21 = (f32[40,1,1024]{2,0,1:T(8,128)}, f32[40,1,1024]{2,0,1:T(8,128)S(1)}, u32[]{:S(2)}) copy-start(f32[40,1,1024]{2,0,1:T(8,128)S(1)} %collective-permute-done.5) | copy-start | bytes 491524
  87.3 11.2 %copy-start.19 = (f32[40,16,1024]{2,0,1:T(8,128)S(1)}, f32[40,16,1024]{2,0,1:T(8,128)}, u32[]{:S(2)}) copy-start(f32[40,16,1024]{2,0,1:T(8,128)} %copy-done.18) | copy-start | bytes 7864324
  87.3 11.2 %copy-start.27 = (f32[40,1,1024]{2,0,1:T(8,128)S(1)}, f32[40,1,1024]{2,0,1:T(8,128)}, u32[]{:S(2)}) copy-start(f32[40,1,1024]{2,0,1:T(8,128)} %copy-done.26) | copy-start | bytes 491524
  87.3 11.2 %copy-start.29 = (f32[40,1,1024]{2,0,1:T(8,128)S(1)}, f32[40,1,1024]{2,0,1:T(8,128)}, u32[]{:S(2)}) copy-start(f32[40,1,1024]{2,0,1:T(8,128)} %copy-done.28) | copy-start | bytes 491524
  87.4 8.9 %collective-permute-start.6 = (f32[40,1,1024]{2,0,1:T(8,128)S(1)}, f32[40,1,1024]{2,0,1:T(8,128)S(1)}, u32[]{:S(2)}, u32[]{:S(2)}) collective-permute-start(f32[40,1,1024]{2,0,1:T(8,128)S(1)} %get-tuple-element.124), channel_id=1, source_target_pairs={{2,0},{4,2},{6,4},{8,6},{10,8},{12,10},{14,12},{16,14},{18,16},{20... | collective-permute-start | bytes 491528 | tf_op jit(solution)/shard_map/ppermute | solution.py:20
  88.9 9.6 %collective-permute-start.7 = (f32[40,1,1024]{2,0,1:T(8,128)S(1)}, f32[40,1,1024]{2,0,1:T(8,128)S(1)}, u32[]{:S(2)}, u32[]{:S(2)}) collective-permute-start(f32[40,1,1024]{2,0,1:T(8,128)S(1)} %get-tuple-element.125), channel_id=1, source_target_pairs={{0,2},{2,4},{4,6},{6,8},{8,10},{10,12},{12,14},{14,16},{16,18},{18... | collective-permute-start | bytes 491528 | tf_op jit(solution)/shard_map/ppermute | solution.py:17
  183.8 19.5 %copy-start.4 = (f32[5,16,8,1024]{3,2,0,1:T(8,128)S(1)}, f32[5,16,8,1024]{3,2,0,1:T(8,128)}, u32[]{:S(2)}) copy-start(f32[5,16,8,1024]{3,2,0,1:T(8,128)} %copy-done.3) | copy-start | bytes 7864324
  183.8 19.5 %copy-start.7 = (f32[40,16,1024]{2,0,1:T(8,128)S(1)}, f32[40,16,1024]{2,0,1:T(8,128)}, u32[]{:S(2)}) copy-start(f32[40,16,1024]{2,0,1:T(8,128)} %copy-done.6) | copy-start | bytes 7864324
  183.8 19.5 %copy-start.17 = (f32[40,16,1024]{2,0,1:T(8,128)S(1)}, f32[40,16,1024]{2,0,1:T(8,128)}, u32[]{:S(2)}) copy-start(f32[40,16,1024]{2,0,1:T(8,128)} %get-tuple-element.109) | copy-start | bytes 7864324
  197.4 68.4 %copy-start.9 = (f32[40,16,1024]{2,0,1:T(8,128)}, f32[40,16,1024]{2,0,1:T(8,128)S(1)}, u32[]{:S(2)}) copy-start(f32[40,16,1024]{2,0,1:T(8,128)S(1)} %multiply_add_fusion.2) | copy-start | bytes 7864324
  197.4 11.7 %collective-permute-start.8 = (f32[40,1,1024]{2,0,1:T(8,128)S(1)}, f32[40,1,1024]{2,0,1:T(8,128)S(1)}, u32[]{:S(2)}, u32[]{:S(2)}) collective-permute-start(f32[40,1,1024]{2,0,1:T(8,128)S(1)} %get-tuple-element.118), channel_id=1, source_target_pairs={{2,0},{4,2},{6,4},{8,6},{10,8},{12,10},{14,12},{16,14},{18,16},{20... | collective-permute-start | bytes 491528 | tf_op jit(solution)/shard_map/ppermute | solution.py:20
  198.7 10.4 %collective-permute-start.9 = (f32[40,1,1024]{2,0,1:T(8,128)S(1)}, f32[40,1,1024]{2,0,1:T(8,128)S(1)}, u32[]{:S(2)}, u32[]{:S(2)}) collective-permute-start(f32[40,1,1024]{2,0,1:T(8,128)S(1)} %get-tuple-element.119), channel_id=1, source_target_pairs={{0,2},{2,4},{4,6},{6,8},{8,10},{10,12},{12,14},{14,16},{16,18},{18... | collective-permute-start | bytes 491528 | tf_op jit(solution)/shard_map/ppermute | solution.py:17
  203.3 5.8 %copy-start.36 = (f32[40]{0:T(128)S(1)}, f32[40]{0:T(128)}, u32[]{:S(2)}) copy-start(f32[40]{0:T(128)} %copy-done.35) | copy-start | bytes 484
  209.1 56.6 %copy-start.11 = (f32[40,16,1024]{2,0,1:T(8,128)}, f32[40,16,1024]{2,0,1:T(8,128)S(1)}, u32[]{:S(2)}) copy-start(f32[40,16,1024]{2,0,1:T(8,128)S(1)} %multiply_add_fusion.1) | copy-start | bytes 7864324
  210.6 55.1 %copy-start.13 = (f32[40,16,1024]{2,0,1:T(8,128)}, f32[40,16,1024]{2,0,1:T(8,128)S(1)}, u32[]{:S(2)}) copy-start(f32[40,16,1024]{2,0,1:T(8,128)S(1)} %fusion.14) | copy-start | bytes 7864324
  210.6 11.8 %collective-permute-start.10 = (f32[40,1,1024]{2,0,1:T(8,128)S(1)}, f32[40,1,1024]{2,0,1:T(8,128)S(1)}, u32[]{:S(2)}, u32[]{:S(2)}) collective-permute-start(f32[40,1,1024]{2,0,1:T(8,128)S(1)} %get-tuple-element.116), channel_id=1, source_target_pairs={{2,0},{4,2},{6,4},{8,6},{10,8},{12,10},{14,12},{16,14},{18,16},{20... | collective-permute-start | bytes 491528 | tf_op jit(solution)/shard_map/ppermute | solution.py:20
  211.9 10.5 %collective-permute-start.11 = (f32[40,1,1024]{2,0,1:T(8,128)S(1)}, f32[40,1,1024]{2,0,1:T(8,128)S(1)}, u32[]{:S(2)}, u32[]{:S(2)}) collective-permute-start(f32[40,1,1024]{2,0,1:T(8,128)S(1)} %get-tuple-element.117), channel_id=1, source_target_pairs={{0,2},{2,4},{4,6},{6,8},{8,10},{10,12},{12,14},{14,16},{16,18},{18... | collective-permute-start | bytes 491528 | tf_op jit(solution)/shard_map/ppermute | solution.py:17
  216.5 13.7 %collective-permute-start.16 = (f32[40,1,1024]{2,0,1:T(8,128)S(1)}, f32[40,1,1024]{2,0,1:T(8,128)S(1)}, u32[]{:S(2)}, u32[]{:S(2)}) collective-permute-start(f32[40,1,1024]{2,0,1:T(8,128)S(1)} %get-tuple-element.122), channel_id=1, source_target_pairs={{2,0},{4,2},{6,4},{8,6},{10,8},{12,10},{14,12},{16,14},{18,16},{20... | collective-permute-start | bytes 491528 | tf_op jit(solution)/shard_map/ppermute | solution.py:20
  217.8 12.4 %collective-permute-start.17 = (f32[40,1,1024]{2,0,1:T(8,128)S(1)}, f32[40,1,1024]{2,0,1:T(8,128)S(1)}, u32[]{:S(2)}, u32[]{:S(2)}) collective-permute-start(f32[40,1,1024]{2,0,1:T(8,128)S(1)} %get-tuple-element.123), channel_id=1, source_target_pairs={{0,2},{2,4},{4,6},{6,8},{8,10},{10,12},{12,14},{14,16},{16,18},{18... | collective-permute-start | bytes 491528 | tf_op jit(solution)/shard_map/ppermute | solution.py:17
  223.9 8.7 %collective-permute-start.12 = (f32[40,1,1024]{2,0,1:T(8,128)S(1)}, f32[40,1,1024]{2,0,1:T(8,128)S(1)}, u32[]{:S(2)}, u32[]{:S(2)}) collective-permute-start(f32[40,1,1024]{2,0,1:T(8,128)S(1)} %get-tuple-element.114), channel_id=1, source_target_pairs={{2,0},{4,2},{6,4},{8,6},{10,8},{12,10},{14,12},{16,14},{18,16},{20... | collective-permute-start | bytes 491528 | tf_op jit(solution)/shard_map/ppermute | solution.py:20
  225.2 9.3 %collective-permute-start.13 = (f32[40,1,1024]{2,0,1:T(8,128)S(1)}, f32[40,1,1024]{2,0,1:T(8,128)S(1)}, u32[]{:S(2)}, u32[]{:S(2)}) collective-permute-start(f32[40,1,1024]{2,0,1:T(8,128)S(1)} %get-tuple-element.115), channel_id=1, source_target_pairs={{0,2},{2,4},{4,6},{6,8},{8,10},{10,12},{12,14},{14,16},{16,18},{18... | collective-permute-start | bytes 491528 | tf_op jit(solution)/shard_map/ppermute | solution.py:17
  237.8 17.2 %copy-start.15 = (f32[40,16,1024]{2,0,1:T(8,128)}, f32[40,16,1024]{2,0,1:T(8,128)S(1)}, u32[]{:S(2)}) copy-start(f32[40,16,1024]{2,0,1:T(8,128)S(1)} %get-tuple-element.182) | copy-start | bytes 7864324
  237.9 17.2 %copy-start.16 = (f32[40,16,1024]{2,0,1:T(8,128)}, f32[40,16,1024]{2,0,1:T(8,128)S(1)}, u32[]{:S(2)}) copy-start(f32[40,16,1024]{2,0,1:T(8,128)S(1)} %get-tuple-element.181) | copy-start | bytes 7864324
  237.9 15.7 %collective-permute-start.18 = (f32[40,1,1024]{2,0,1:T(8,128)S(1)}, f32[40,1,1024]{2,0,1:T(8,128)S(1)}, u32[]{:S(2)}, u32[]{:S(2)}) collective-permute-start(f32[40,1,1024]{2,0,1:T(8,128)S(1)} %get-tuple-element.120), channel_id=1, source_target_pairs={{2,0},{4,2},{6,4},{8,6},{10,8},{12,10},{14,12},{16,14},{18,16},{20... | collective-permute-start | bytes 491528 | tf_op jit(solution)/shard_map/ppermute | solution.py:20
  239.2 14.4 %collective-permute-start.19 = (f32[40,1,1024]{2,0,1:T(8,128)S(1)}, f32[40,1,1024]{2,0,1:T(8,128)S(1)}, u32[]{:S(2)}, u32[]{:S(2)}) collective-permute-start(f32[40,1,1024]{2,0,1:T(8,128)S(1)} %get-tuple-element.121), channel_id=1, source_target_pairs={{0,2},{2,4},{4,6},{6,8},{8,10},{10,12},{12,14},{14,16},{16,18},{18... | collective-permute-start | bytes 491528 | tf_op jit(solution)/shard_map/ppermute | solution.py:17
  246.1 18.0 %collective-permute-start.14 = (f32[40,1,1024]{2,0,1:T(8,128)S(1)}, f32[40,1,1024]{2,0,1:T(8,128)}, u32[]{:S(2)}, u32[]{:S(2)}) collective-permute-start(f32[40,1,1024]{2,0,1:T(8,128)S(1)} %get-tuple-element.112), channel_id=1, source_target_pairs={{2,0},{4,2},{6,4},{8,6},{10,8},{12,10},{14,12},{16,14},{18,16},{20... | collective-permute-start | bytes 491528 | tf_op jit(solution)/shard_map/ppermute | solution.py:20
  247.4 16.7 %collective-permute-start.15 = (f32[40,1,1024]{2,0,1:T(8,128)S(1)}, f32[40,1,1024]{2,0,1:T(8,128)}, u32[]{:S(2)}, u32[]{:S(2)}) collective-permute-start(f32[40,1,1024]{2,0,1:T(8,128)S(1)} %get-tuple-element.113), channel_id=1, source_target_pairs={{0,2},{2,4},{4,6},{6,8},{8,10},{10,12},{12,14},{14,16},{16,18},{18... | collective-permute-start | bytes 491528 | tf_op jit(solution)/shard_map/ppermute | solution.py:17
  256.5 7.8 %collective-permute-start.20 = (f32[40,1,1024]{2,0,1:T(8,128)S(1)}, f32[40,1,1024]{2,0,1:T(8,128)}, u32[]{:S(2)}, u32[]{:S(2)}) collective-permute-start(f32[40,1,1024]{2,0,1:T(8,128)S(1)} %get-tuple-element.110), channel_id=1, source_target_pairs={{2,0},{4,2},{6,4},{8,6},{10,8},{12,10},{14,12},{16,14},{18,16},{20... | collective-permute-start | bytes 491528 | tf_op jit(solution)/shard_map/ppermute | solution.py:20
  257.8 7.9 %collective-permute-start.21 = (f32[40,1,1024]{2,0,1:T(8,128)S(1)}, f32[40,1,1024]{2,0,1:T(8,128)}, u32[]{:S(2)}, u32[]{:S(2)}) collective-permute-start(f32[40,1,1024]{2,0,1:T(8,128)S(1)} %get-tuple-element.111), channel_id=1, source_target_pairs={{0,2},{2,4},{4,6},{6,8},{8,10},{10,12},{12,14},{14,16},{16,18},{18... | collective-permute-start | bytes 491528 | tf_op jit(solution)/shard_map/ppermute | solution.py:17
  264.2 124.1 %copy-start.34 = (f32[40,9]{1,0:T(8,128)S(1)}, f32[40,9]{1,0:T(8,128)}, u32[]{:S(2)}) copy-start(f32[40,9]{1,0:T(8,128)} %copy-done.33) | copy-start | bytes 4324
  264.2 127.0 %copy-start.25 = (f32[40,9]{0,1:T(8,128)S(1)}, f32[40,9]{0,1:T(8,128)}, u32[]{:S(2)}) copy-start(f32[40,9]{0,1:T(8,128)} %copy-done.24) | copy-start | bytes 4324
  264.2 133.2 %copy-start.31 = (f32[9,9]{1,0:T(8,128)S(1)}, f32[9,9]{1,0:T(8,128)}, u32[]{:S(2)}) copy-start(f32[9,9]{1,0:T(8,128)} %constant.100.clone) | copy-start | bytes 976
  290.3 5.6 %copy-start.50 = (f32[40]{0:T(128)}, f32[40]{0:T(128)S(1)}, u32[]{:S(2)}) copy-start(f32[40]{0:T(128)S(1)} %get-tuple-element.75) | copy-start | bytes 484
  290.3 5.6 %copy-start.51 = (f32[40]{0:T(128)}, f32[40]{0:T(128)S(1)}, u32[]{:S(2)}) copy-start(f32[40]{0:T(128)S(1)} %get-tuple-element.76) | copy-start | bytes 484
  290.3 7.0 %copy-start.45 = (f32[40]{0:T(128)}, f32[40]{0:T(128)S(1)}, u32[]{:S(2)}) copy-start(f32[40]{0:T(128)S(1)} %get-tuple-element.83) | copy-start | bytes 484
  290.3 7.0 %copy-start.46 = (f32[40]{0:T(128)}, f32[40]{0:T(128)S(1)}, u32[]{:S(2)}) copy-start(f32[40]{0:T(128)S(1)} %get-tuple-element.84) | copy-start | bytes 484
  290.3 8.4 %copy-start.44 = (f32[40]{0:T(128)}, f32[40]{0:T(128)S(1)}, u32[]{:S(2)}) copy-start(f32[40]{0:T(128)S(1)} %get-tuple-element.82) | copy-start | bytes 484
  290.3 8.4 %copy-start.47 = (f32[40]{0:T(128)}, f32[40]{0:T(128)S(1)}, u32[]{:S(2)}) copy-start(f32[40]{0:T(128)S(1)} %get-tuple-element.85) | copy-start | bytes 484
  290.4 9.7 %copy-start.48 = (f32[40]{0:T(128)}, f32[40]{0:T(128)S(1)}, u32[]{:S(2)}) copy-start(f32[40]{0:T(128)S(1)} %get-tuple-element.86) | copy-start | bytes 484
  290.4 9.7 %copy-start.49 = (f32[40]{0:T(128)}, f32[40]{0:T(128)S(1)}, u32[]{:S(2)}) copy-start(f32[40]{0:T(128)S(1)} %get-tuple-element.87) | copy-start | bytes 484
  290.4 11.0 %copy-start.42 = (f32[40]{0:T(128)}, f32[40]{0:T(128)S(1)}, u32[]{:S(2)}) copy-start(f32[40]{0:T(128)S(1)} %get-tuple-element.80) | copy-start | bytes 484
  290.4 11.0 %copy-start.43 = (f32[40]{0:T(128)}, f32[40]{0:T(128)S(1)}, u32[]{:S(2)}) copy-start(f32[40]{0:T(128)S(1)} %get-tuple-element.81) | copy-start | bytes 484
  422.1 24.2 %copy-start.10 = (f32[40,16,1024]{2,0,1:T(8,128)S(1)}, f32[40,16,1024]{2,0,1:T(8,128)}, u32[]{:S(2)}) copy-start(f32[40,16,1024]{2,0,1:T(8,128)} %copy-done.9) | copy-start | bytes 7864324
  422.2 24.2 %copy-start.12 = (f32[40,16,1024]{2,0,1:T(8,128)S(1)}, f32[40,16,1024]{2,0,1:T(8,128)}, u32[]{:S(2)}) copy-start(f32[40,16,1024]{2,0,1:T(8,128)} %copy-done.11) | copy-start | bytes 7864324
  422.2 24.2 %copy-start.14 = (f32[40,16,1024]{2,0,1:T(8,128)S(1)}, f32[40,16,1024]{2,0,1:T(8,128)}, u32[]{:S(2)}) copy-start(f32[40,16,1024]{2,0,1:T(8,128)} %copy-done.13) | copy-start | bytes 7864324
  446.5 15.8 %copy-start.1 = (bf16[80,136]{0,1:T(8,128)(2,1)S(1)}, bf16[80,136]{0,1:T(8,128)(2,1)}, u32[]{:S(2)}) copy-start(bf16[80,136]{0,1:T(8,128)(2,1)} %param.13) | copy-start | bytes 65284
  (32 other events, 96.6 us)
Sparse Core Ops, SparseCore 0:
  17.1 15.7 reduce-scatter.1
where the time goes:
time: 471 us; the launch traced here: 469 us
  blocking collectives  153 us (32%)
  other arithmetic  124 us (26%)
  starting transfers between devices  71.4 us (15%)
  local copies, waits for them, and re-layouts  55.5 us (12%)
  waiting for transfers between devices  41.9 us (9%)
  between operations  16.7 us (4%)
  matrix products  7.1 us (2%)
    psum x2, blocking collectives, shards(): gram = lax.psum(gram, 'tile')  153 us
    ppermute x11, starting transfers between devices, extended(): lax.ppermute(lax.slice_in_dim(block, block.shape[dim] - width, None, axis...  56.9 us
    add x3, other arithmetic, combine(): total = total + coef[:, index, None, None] * vectors[index]  38.5 us
    reduce_sum x3, other arithmetic, inner_table(): jnp.sum(vectors[first] * vectors[second], axis=(1, 2))  30.2 us
    unnamed x180, local copies, waits for them, and re-layouts  29.2 us
    mul x7, other arithmetic, stencil_rows(): return weight_col * beside_all  20.1 us
    ppermute x11, waiting for transfers between devices, extended(): lax.ppermute(lax.slice_in_dim(block, block.shape[dim] - width, None, axis...  16.6 us
    reduce_scatter x1, waiting for transfers between devices, shards(): lax.psum_scatter(jnp.dot(own_cols, flat, preferred_element_type=jnp.float...  15.9 us
  transfers between devices with their start and end apart: 23, of which 12 were waited for; matrix products, arithmetic and copies ran while one was open for 2% of the time, Pallas kernels for 0%

commit v1 on v0

--- a/solution.py
+++ b/solution.py
@@ -1,12 +1,23 @@
+import functools
 import jax
 import jax.numpy as jnp
 import numpy as np
 from jax import lax
 from jax.sharding import PartitionSpec as P
+from jax.lax import all_gather
 
 S = 4
 BLOCKS = 2
 highest = lax.Precision.HIGHEST
+
+
+def _answer_lane(sheet, axis_name):
+    t_next = all_gather(sheet, axis_name=axis_name)
+    item_now = jnp.sum(t_next, 0)
+    return item_now
+
+
+vector_guide = functools.partial(_answer_lane, axis_name="tile")
 
 
 def extended(block, sides, width):
@@ -95,7 +106,7 @@
             current = stencil_rows(current, weight_col)
             vectors.append(current)
         gram = inner_table(vectors)
-        gram = lax.psum(gram, "tile")
+        gram = vector_guide(gram)
         p_coef = jnp.zeros((mode_count, width), jnp.float32).at[:, 0].set(1.0)
         r_coef = jnp.zeros((mode_count, width), jnp.float32).at[:, S + 1].set(1.0)
         x_coef = jnp.zeros((mode_count, width), jnp.float32)

time: 471 us -> 581 us (1.23)
  blocking collectives: 153 us -> 246 us
  other arithmetic: 124 us -> 131 us
  local copies, waits for them, and re-layouts: 55.5 us -> 62 us
    all_gather x0 -> x2, blocking collectives: none -> 246 us  [_answer_lane(): t_next = all_gather(sheet, axis_name=axis_name)]
    psum x2 -> x0, blocking collectives: 153 us -> none  [shards(): gram = lax.psum(gram, 'tile')]
    reduce_sum x0 -> x2, other arithmetic: none -> 7.39 us  [_answer_lane(): item_now = jnp.sum(t_next, 0)]
    unnamed x180 -> x162, local copies, waits for them, and re-layouts: 29.2 us -> 30.2 us
  transfers between devices with their start and end apart: 23 -> 23, of which waited for: 12 -> 15; matrix products, arithmetic and copies ran while one was open for 2% -> 2% of each run, Pallas kernels for 0% -> 0%
where the time goes in v1:
time: 581 us; the launch traced here: 579 us
  blocking collectives  246 us (42%)
  other arithmetic  131 us (23%)
  starting transfers between devices  72.5 us (12%)
  local copies, waits for them, and re-layouts  62 us (11%)
  waiting for transfers between devices  44.1 us (8%)
  between operations  16.4 us (3%)
  matrix products  7.1 us (1%)
    all_gather x2, blocking collectives, _answer_lane(): t_next = all_gather(sheet, axis_name=axis_name)  246 us
    ppermute x11, starting transfers between devices, extended(): lax.ppermute(lax.slice_in_dim(block, block.shape[dim] - width, None, axis...  58 us
    add x3, other arithmetic, combine(): total = total + coef[:, index, None, None] * vectors[index]  38.5 us
    unnamed x162, local copies, waits for them, and re-layouts  30.2 us
    reduce_sum x3, other arithmetic, inner_table(): jnp.sum(vectors[first] * vectors[second], axis=(1, 2))  30.1 us
    mul x7, other arithmetic, stencil_rows(): return weight_col * beside_all  20.1 us
    ppermute x11, waiting for transfers between devices, extended(): lax.ppermute(lax.slice_in_dim(block, block.shape[dim] - width, None, axis...  19.6 us
    another operation x14, local copies, waits for them, and re-layouts, inner_table(): rows_list.append(jnp.stack(entries, axis=1))  16.7 us
  transfers between devices with their start and end apart: 23, of which 15 were waited for; matrix products, arithmetic and copies ran while one was open for 2% of the time, Pallas kernels for 0%

profile of v1, /device:TPU:0, one launch (start us, length us, event | category | flops | bytes accessed | tf_op | source)
XLA Modules:
  0.0 578.8 jit_solution(1811130278773603440)
XLA Ops:
  7.2 2.0 pad.144
  9.2 2.9 copy.241
  12.1 4.9 fusion.44
  17.0 15.9 %reduce-scatter.2.cloned.1.call-done = f32[40,16384]{1,0:T(8,128)} async-done(((f32[80,16384]{1,0:T(8,128)}), f32[40,16384]{1,0:T(8,128)}) %reduce-scatter.2.cloned.1.call-update) | async-done | bytes 2621456 | tf_op jit(solution)/shard_map/reduce_scatter | solution.py:84
  32.9 2.0 copy.257
  36.3 4.6 collective-permute-start.1
  40.9 2.4 collective-permute-done
  43.3 4.5 collective-permute-done.1
  47.8 1.4 fusion.2
  52.1 5.0 collective-permute-start.3
  59.8 2.0 collective-permute-done.3
  61.8 5.5 fusion.5
  69.5 5.0 collective-permute-start.5
  74.8 2.3 collective-permute-done.4
  77.1 4.5 collective-permute-done.5
  81.7 5.6 fusion.8
  87.4 1.6 collective-permute-start.6
  88.9 4.9 collective-permute-start.7
  94.2 2.2 collective-permute-done.6
  96.3 2.2 collective-permute-done.7
  98.5 5.5 multiply_reduce_fusion.45
  105.2 118.7 %all-gather = f32[640,9,9]{2,1,0:T(8,128)} all-gather(f32[40,9,9]{2,1,0:T(8,128)} %copy.15), channel_id=2, replica_groups=mesh['tile'=16,'lev'=2] {'tile'}, dimensions={0}, use_global_device_ids=true | all-gather | bytes 220320 | tf_op jit(solution)/shard_map/all_gather | solution.py:15
  223.9 3.7 reduce_sum.568
  233.0 13.7 %multiply_add_fusion.2 = f32[40,16,1024]{2,0,1:T(8,128)S(1)} fusion(f32[40,16,1024]{2,0,1:T(8,128)} %copy-done.6, f32[40,16,1024]{2,0,1:T(8,128)} %get-tuple-element.109, f32[40]{0:T(128)S(1)} %get-tuple-element.162, f32[40]{0:T(128)S(1)} %get-tuple-element.163, f32[40]{0:T(128)S(1)} %get-tuple-element.164, f32[40]{0:T(128)S(1)} %get-tuple-element.165, ...), kind=kLoop, calls=%fused_computation.137 | loop fusion | flops 19005440 | bytes 13764160 | tf_op jit(solution)/shard_map/add | solution.py:60
  246.7 1.3 collective-permute-start.8
  248.0 5.4 collective-permute-start.9
  253.4 5.8 multiply_add_fusion.1
  259.3 1.4 fusion.14
  262.0 5.9 %collective-permute-start.11 = (f32[40,1,1024]{2,0,1:T(8,128)S(1)}, f32[40,1,1024]{2,0,1:T(8,128)S(1)}, u32[]{:S(2)}, u32[]{:S(2)}) collective-permute-start(f32[40,1,1024]{2,0,1:T(8,128)S(1)} %get-tuple-element.117), channel_id=1, source_target_pairs={{0,2},{2,4},{4,6},{6,8},{8,10},{10,12},{12,14},{14,16},{16,18},{18... | collective-permute-start | bytes 491528 | tf_op jit(solution)/shard_map/ppermute | solution.py:28
  269.3 5.4 collective-permute-start.17
  275.9 1.4 fusion.17
  278.6 5.0 collective-permute-start.13
  283.7 1.3 collective-permute-done.12
  285.0 3.2 collective-permute-done.13
  288.2 3.3 fusion.20
  292.9 5.0 collective-permute-start.19
  299.2 6.1 %collective-permute-start.15 = (f32[40,1,1024]{2,0,1:T(8,128)S(1)}, f32[40,1,1024]{2,0,1:T(8,128)}, u32[]{:S(2)}, u32[]{:S(2)}) collective-permute-start(f32[40,1,1024]{2,0,1:T(8,128)S(1)} %get-tuple-element.113), channel_id=1, source_target_pairs={{0,2},{2,4},{4,6},{6,8},{8,10},{10,12},{12,14},{14,16},{16,18},{18... | collective-permute-start | bytes 491528 | tf_op jit(solution)/shard_map/ppermute | solution.py:28
  305.9 1.4 fusion.29
  307.4 1.5 copy-done.20
  310.2 5.7 collective-permute-start.21
  316.6 1.4 collective-permute-done.21
  318.0 24.4 %multiply_reduce_fusion = (f32[40]{0:T(128)}, f32[40]{0:T(128)}, f32[40]{0:T(128)}, f32[40]{0:T(128)}, f32[40]{0:T(128)}, /*index=5*/f32[40]{0:T(128)}, f32[40]{...) fusion(f32[40,16,1024]{2,0,1:T(8,128)} %copy-done.20, ...), kind=kLoop, calls=%fused_computation.91 | loop fusion | flops 70777080 | bytes 21961920 | tf_op jit(solution)/shard_map/reduce_sum | solution.py:69
  342.4 1.3 stack.467
  343.8 1.4 stack.464
  346.4 1.4 stack.455
  347.8 2.5 stack.449
  350.3 2.4 stack.442
  352.8 2.5 stack.434
  355.3 1.8 stack.425
  357.1 1.9 stack.415
  363.4 126.9 %all-gather.1 = f32[640,9,9]{2,1,0:T(8,128)} all-gather(f32[40,9,9]{2,1,0:T(8,128)} %copy.23), channel_id=3, replica_groups=mesh['tile'=16,'lev'=2] {'tile'}, dimensions={0}, use_global_device_ids=true | all-gather | bytes 220320 | tf_op jit(solution)/shard_map/all_gather | solution.py:15
  490.3 3.7 reduce_sum.739
  495.1 1.4 multiply_reduce_fusion.66
  496.5 1.4 copy.121
  497.9 1.4 multiply_reduce_fusion.83
  503.4 1.4 copy.130
  509.2 1.4 copy.143
  518.4 1.4 copy.157
  519.7 1.4 copy.161
  524.0 1.4 copy.170
  532.1 19.1 %multiply_add_fusion = f32[40,16,1024]{2,0,1:T(8,128)} fusion(f32[40,16,1024]{2,0,1:T(8,128)} %get-tuple-element.108, f32[40,16,1024]{2,0,1:T(8,128)} %copy-done.15, f32[40,16,1024]{2,0,1:T(8,128)} %copy-done.11, f32[40,16,1024]{2,0,1:T(8,128)} %get-tuple-element.107, f32[40,16,1024]{2,0,1:T(8,128)} %copy-done.16, f32[40,16,1024]{2,0,1:T(8,128)} %copy-done.13, ...), kind=kLoop, calls=%fused_computation.89 | loop fusion | flops 19005440 | bytes 21628480 | tf_op jit(solution)/shard_map/add | solution.py:60
  551.3 4.9 copy.26
  556.4 12.6 %add_add_fusion = f32[40,16,1024]{2,0,1:T(8,128)S(1)} fusion(f32[40,16,1024]{2,0,1:T(8,128)} %get-tuple-element.108, f32[40,16,1024]{2,0,1:T(8,128)} %copy-done.15, f32[40,16,1024]{2,0,1:T(8,128)S(1)} %copy-done.12, f32[40,16,1024]{2,0,1:T(8,128)} %get-tuple-element.107, f32[40,16,1024]{2,0,1:T(8,128)} %copy-done.16, f32[40,16,1024]{2,0,1:T(8,128)S(1)} %copy-done.14, ...), kind=kLoop, calls=%fused_computation.90 | loop fusion | flops 38666240 | bytes 32771040 | tf_op jit(solution)/shard_map/add | solution.py:122
  569.0 3.0 copy.25
  (289 shorter events, 58.0 us)
Async XLA Ops:
  7.2 25.7 %reduce-scatter.2.cloned.1.call-start = ((), (), s32[]{:S(2)}) async-start(), calls=%async_computation.1 | async-start | bytes 7864320 | tf_op jit(solution)/shard_map/reduce_scatter | solution.py:84
  32.9 8.0 %copy-start.62 = (f32[40]{0:T(128)S(1)}, f32[40]{0:T(128)}, u32[]{:S(2)}) copy-start(f32[40]{0:T(128)} %param.14) | copy-start | bytes 484
  34.9 14.3 %copy-start.3 = (f32[5,16,8,1024]{3,2,0,1:T(8,128)}, f32[5,16,8,1024]{3,2,0,1:T(8,128)S(1)}, u32[]{:S(2)}) copy-start(f32[5,16,8,1024]{3,2,0,1:T(8,128)S(1)} %copy.257) | copy-start | bytes 7864324
  35.0 8.3 %collective-permute-start = (f32[40,1,1024]{2,0,1:T(8,128)S(1)}, f32[40,1,1024]{2,0,1:T(8,128)S(1)}, u32[]{:S(2)}, u32[]{:S(2)}) collective-permute-start(f32[40,1,1024]{2,0,1:T(8,128)S(1)} %get-tuple-element.130), channel_id=1, source_target_pairs={{2,0},{4,2},{6,4},{8,6},{10,8},{12,10},{14,12},{16,14},{18,16},{20... | collective-permute-start | bytes 491528 | tf_op jit(solution)/shard_map/ppermute | solution.py:31
  36.3 11.5 %collective-permute-start.1 = (f32[40,1,1024]{2,0,1:T(8,128)S(1)}, f32[40,1,1024]{2,0,1:T(8,128)S(1)}, u32[]{:S(2)}, u32[]{:S(2)}) collective-permute-start(f32[40,1,1024]{2,0,1:T(8,128)S(1)} %get-tuple-element.131), channel_id=1, source_target_pairs={{0,2},{2,4},{4,6},{6,8},{8,10},{10,12},{12,14},{14,16},{16,18},{18... | collective-permute-start | bytes 491528 | tf_op jit(solution)/shard_map/ppermute | solution.py:28
  40.9 192.1 %copy-start.35 = (f32[40]{0:T(128)}, f32[40]{0:T(128)S(1)}, u32[]{:S(2)}) copy-start(f32[40]{0:T(128)S(1)} %add_divide_fusion) | copy-start | bytes 484
  50.8 9.0 %collective-permute-start.2 = (f32[40,1,1024]{2,0,1:T(8,128)}, f32[40,1,1024]{2,0,1:T(8,128)S(1)}, u32[]{:S(2)}, u32[]{:S(2)}) collective-permute-start(f32[40,1,1024]{2,0,1:T(8,128)} %get-tuple-element.128), channel_id=1, source_target_pairs={{2,0},{4,2},{6,4},{8,6},{10,8},{12,10},{14,12},{16,14},{18,16},{20... | collective-permute-start | bytes 491528 | tf_op jit(solution)/shard_map/ppermute | solution.py:31
  52.1 9.7 %collective-permute-start.3 = (f32[40,1,1024]{2,0,1:T(8,128)S(1)}, f32[40,1,1024]{2,0,1:T(8,128)S(1)}, u32[]{:S(2)}, u32[]{:S(2)}) collective-permute-start(f32[40,1,1024]{2,0,1:T(8,128)S(1)} %get-tuple-element.129), channel_id=1, source_target_pairs={{0,2},{2,4},{4,6},{6,8},{8,10},{10,12},{12,14},{14,16},{16,18},{18... | collective-permute-start | bytes 491528 | tf_op jit(solution)/shard_map/ppermute | solution.py:28
  59.6 170.9 %copy-start.39 = (f32[9]{0:T(128)}, f32[9]{0:T(128)S(1)}, u32[]{:S(2)}) copy-start(f32[9]{0:T(128)S(1)} %scatter.16) | copy-start | bytes 112
  59.6 14.9 %copy-start.30 = (f32[9,9]{1,0:T(8,128)S(1)}, f32[9,9]{1,0:T(8,128)}, u32[]{:S(2)}) copy-start(f32[9,9]{1,0:T(8,128)} %constant.100.clone) | copy-start | bytes 976
  59.8 7.6 %copy-start.26 = (f32[40,1,1024]{2,0,1:T(8,128)}, f32[40,1,1024]{2,0,1:T(8,128)S(1)}, u32[]{:S(2)}) copy-start(f32[40,1,1024]{2,0,1:T(8,128)S(1)} %collective-permute-done.2) | copy-start | bytes 491524
  61.8 5.5 copy-start.28
  67.4 7.3 %copy-start.6 = (f32[40,16,1024]{2,0,1:T(8,128)}, f32[40,16,1024]{2,0,1:T(8,128)S(1)}, u32[]{:S(2)}) copy-start(f32[40,16,1024]{2,0,1:T(8,128)S(1)} %fusion.5) | copy-start | bytes 7864324
  68.2 9.0 %collective-permute-start.4 = (f32[40,1,1024]{2,0,1:T(8,128)}, f32[40,1,1024]{2,0,1:T(8,128)S(1)}, u32[]{:S(2)}, u32[]{:S(2)}) collective-permute-start(f32[40,1,1024]{2,0,1:T(8,128)} %get-tuple-element.126), channel_id=1, source_target_pairs={{2,0},{4,2},{6,4},{8,6},{10,8},{12,10},{14,12},{16,14},{18,16},{20... | collective-permute-start | bytes 491528 | tf_op jit(solution)/shard_map/ppermute | solution.py:31
  69.5 12.2 %collective-permute-start.5 = (f32[40,1,1024]{2,0,1:T(8,128)}, f32[40,1,1024]{2,0,1:T(8,128)S(1)}, u32[]{:S(2)}, u32[]{:S(2)}) collective-permute-start(f32[40,1,1024]{2,0,1:T(8,128)} %get-tuple-element.127), channel_id=1, source_target_pairs={{0,2},{2,4},{4,6},{6,8},{8,10},{10,12},{12,14},{14,16},{16,18},{18... | collective-permute-start | bytes 491528 | tf_op jit(solution)/shard_map/ppermute | solution.py:28
  74.7 157.5 %copy-start.24 = (f32[40,9]{0,1:T(8,128)}, f32[40,9]{0,1:T(8,128)S(1)}, u32[]{:S(2)}) copy-start(f32[40,9]{0,1:T(8,128)S(1)} %convolution_subtract_fusion.6) | copy-start | bytes 4324
  74.8 154.2 %copy-start.33 = (f32[40,9]{1,0:T(8,128)}, f32[40,9]{1,0:T(8,128)S(1)}, u32[]{:S(2)}) copy-start(f32[40,9]{1,0:T(8,128)S(1)} %copy.44) | copy-start | bytes 4324
  74.8 19.1 %copy-start.2 = (f32[40,16384]{1,0:T(8,128)S(1)}, f32[40,16384]{1,0:T(8,128)}, u32[]{:S(2)}) copy-start(f32[40,16384]{1,0:T(8,128)} %reduce-scatter.2.cloned.1.call-done) | copy-start | bytes 7864324
  81.7 171.7 %copy-start.21 = (f32[40,1,1024]{2,0,1:T(8,128)}, f32[40,1,1024]{2,0,1:T(8,128)S(1)}, u32[]{:S(2)}) copy-start(f32[40,1,1024]{2,0,1:T(8,128)S(1)} %collective-permute-done.5) | copy-start | bytes 491524
  87.3 11.2 %copy-start.19 = (f32[40,16,1024]{2,0,1:T(8,128)S(1)}, f32[40,16,1024]{2,0,1:T(8,128)}, u32[]{:S(2)}) copy-start(f32[40,16,1024]{2,0,1:T(8,128)} %copy-done.18) | copy-start | bytes 7864324
  87.3 11.2 %copy-start.27 = (f32[40,1,1024]{2,0,1:T(8,128)S(1)}, f32[40,1,1024]{2,0,1:T(8,128)}, u32[]{:S(2)}) copy-start(f32[40,1,1024]{2,0,1:T(8,128)} %copy-done.26) | copy-start | bytes 491524
  87.3 11.2 %copy-start.29 = (f32[40,1,1024]{2,0,1:T(8,128)S(1)}, f32[40,1,1024]{2,0,1:T(8,128)}, u32[]{:S(2)}) copy-start(f32[40,1,1024]{2,0,1:T(8,128)} %copy-done.28) | copy-start | bytes 491524
  87.4 8.9 %collective-permute-start.6 = (f32[40,1,1024]{2,0,1:T(8,128)S(1)}, f32[40,1,1024]{2,0,1:T(8,128)S(1)}, u32[]{:S(2)}, u32[]{:S(2)}) collective-permute-start(f32[40,1,1024]{2,0,1:T(8,128)S(1)} %get-tuple-element.124), channel_id=1, source_target_pairs={{2,0},{4,2},{6,4},{8,6},{10,8},{12,10},{14,12},{16,14},{18,16},{20... | collective-permute-start | bytes 491528 | tf_op jit(solution)/shard_map/ppermute | solution.py:31
  88.9 9.6 %collective-permute-start.7 = (f32[40,1,1024]{2,0,1:T(8,128)S(1)}, f32[40,1,1024]{2,0,1:T(8,128)S(1)}, u32[]{:S(2)}, u32[]{:S(2)}) collective-permute-start(f32[40,1,1024]{2,0,1:T(8,128)S(1)} %get-tuple-element.125), channel_id=1, source_target_pairs={{0,2},{2,4},{4,6},{6,8},{8,10},{10,12},{12,14},{14,16},{16,18},{18... | collective-permute-start | bytes 491528 | tf_op jit(solution)/shard_map/ppermute | solution.py:28
  233.0 20.4 %copy-start.4 = (f32[5,16,8,1024]{3,2,0,1:T(8,128)S(1)}, f32[5,16,8,1024]{3,2,0,1:T(8,128)}, u32[]{:S(2)}) copy-start(f32[5,16,8,1024]{3,2,0,1:T(8,128)} %copy-done.3) | copy-start | bytes 7864324
  233.0 20.4 %copy-start.7 = (f32[40,16,1024]{2,0,1:T(8,128)S(1)}, f32[40,16,1024]{2,0,1:T(8,128)}, u32[]{:S(2)}) copy-start(f32[40,16,1024]{2,0,1:T(8,128)} %copy-done.6) | copy-start | bytes 7864324
  233.0 20.4 %copy-start.17 = (f32[40,16,1024]{2,0,1:T(8,128)S(1)}, f32[40,16,1024]{2,0,1:T(8,128)}, u32[]{:S(2)}) copy-start(f32[40,16,1024]{2,0,1:T(8,128)} %get-tuple-element.109) | copy-start | bytes 7864324
  246.7 71.3 %copy-start.9 = (f32[40,16,1024]{2,0,1:T(8,128)}, f32[40,16,1024]{2,0,1:T(8,128)S(1)}, u32[]{:S(2)}) copy-start(f32[40,16,1024]{2,0,1:T(8,128)S(1)} %multiply_add_fusion.2) | copy-start | bytes 7864324
  246.7 12.5 %collective-permute-start.8 = (f32[40,1,1024]{2,0,1:T(8,128)S(1)}, f32[40,1,1024]{2,0,1:T(8,128)S(1)}, u32[]{:S(2)}, u32[]{:S(2)}) collective-permute-start(f32[40,1,1024]{2,0,1:T(8,128)S(1)} %get-tuple-element.118), channel_id=1, source_target_pairs={{2,0},{4,2},{6,4},{8,6},{10,8},{12,10},{14,12},{16,14},{18,16},{20... | collective-permute-start | bytes 491528 | tf_op jit(solution)/shard_map/ppermute | solution.py:31
  248.0 11.2 %collective-permute-start.9 = (f32[40,1,1024]{2,0,1:T(8,128)S(1)}, f32[40,1,1024]{2,0,1:T(8,128)S(1)}, u32[]{:S(2)}, u32[]{:S(2)}) collective-permute-start(f32[40,1,1024]{2,0,1:T(8,128)S(1)} %get-tuple-element.119), channel_id=1, source_target_pairs={{0,2},{2,4},{4,6},{6,8},{8,10},{10,12},{12,14},{14,16},{16,18},{18... | collective-permute-start | bytes 491528 | tf_op jit(solution)/shard_map/ppermute | solution.py:28
  253.4 5.8 %copy-start.36 = (f32[40]{0:T(128)S(1)}, f32[40]{0:T(128)}, u32[]{:S(2)}) copy-start(f32[40]{0:T(128)} %copy-done.35) | copy-start | bytes 484
  259.2 58.8 %copy-start.11 = (f32[40,16,1024]{2,0,1:T(8,128)}, f32[40,16,1024]{2,0,1:T(8,128)S(1)}, u32[]{:S(2)}) copy-start(f32[40,16,1024]{2,0,1:T(8,128)S(1)} %multiply_add_fusion.1) | copy-start | bytes 7864324
  260.7 57.3 %copy-start.13 = (f32[40,16,1024]{2,0,1:T(8,128)}, f32[40,16,1024]{2,0,1:T(8,128)S(1)}, u32[]{:S(2)}) copy-start(f32[40,16,1024]{2,0,1:T(8,128)S(1)} %fusion.14) | copy-start | bytes 7864324
  260.7 14.0 %collective-permute-start.10 = (f32[40,1,1024]{2,0,1:T(8,128)S(1)}, f32[40,1,1024]{2,0,1:T(8,128)S(1)}, u32[]{:S(2)}, u32[]{:S(2)}) collective-permute-start(f32[40,1,1024]{2,0,1:T(8,128)S(1)} %get-tuple-element.116), channel_id=1, source_target_pairs={{2,0},{4,2},{6,4},{8,6},{10,8},{12,10},{14,12},{16,14},{18,16},{20... | collective-permute-start | bytes 491528 | tf_op jit(solution)/shard_map/ppermute | solution.py:31
  262.0 13.8 %collective-permute-start.11 = (f32[40,1,1024]{2,0,1:T(8,128)S(1)}, f32[40,1,1024]{2,0,1:T(8,128)S(1)}, u32[]{:S(2)}, u32[]{:S(2)}) collective-permute-start(f32[40,1,1024]{2,0,1:T(8,128)S(1)} %get-tuple-element.117), channel_id=1, source_target_pairs={{0,2},{2,4},{4,6},{6,8},{8,10},{10,12},{12,14},{14,16},{16,18},{18... | collective-permute-start | bytes 491528 | tf_op jit(solution)/shard_map/ppermute | solution.py:28
  268.0 15.7 %collective-permute-start.16 = (f32[40,1,1024]{2,0,1:T(8,128)S(1)}, f32[40,1,1024]{2,0,1:T(8,128)S(1)}, u32[]{:S(2)}, u32[]{:S(2)}) collective-permute-start(f32[40,1,1024]{2,0,1:T(8,128)S(1)} %get-tuple-element.122), channel_id=1, source_target_pairs={{2,0},{4,2},{6,4},{8,6},{10,8},{12,10},{14,12},{16,14},{18,16},{20... | collective-permute-start | bytes 491528 | tf_op jit(solution)/shard_map/ppermute | solution.py:31
  269.3 14.4 %collective-permute-start.17 = (f32[40,1,1024]{2,0,1:T(8,128)S(1)}, f32[40,1,1024]{2,0,1:T(8,128)S(1)}, u32[]{:S(2)}, u32[]{:S(2)}) collective-permute-start(f32[40,1,1024]{2,0,1:T(8,128)S(1)} %get-tuple-element.123), channel_id=1, source_target_pairs={{0,2},{2,4},{4,6},{6,8},{8,10},{10,12},{12,14},{14,16},{16,18},{18... | collective-permute-start | bytes 491528 | tf_op jit(solution)/shard_map/ppermute | solution.py:28
  277.3 7.7 %collective-permute-start.12 = (f32[40,1,1024]{2,0,1:T(8,128)S(1)}, f32[40,1,1024]{2,0,1:T(8,128)S(1)}, u32[]{:S(2)}, u32[]{:S(2)}) collective-permute-start(f32[40,1,1024]{2,0,1:T(8,128)S(1)} %get-tuple-element.114), channel_id=1, source_target_pairs={{2,0},{4,2},{6,4},{8,6},{10,8},{12,10},{14,12},{16,14},{18,16},{20... | collective-permute-start | bytes 491528 | tf_op jit(solution)/shard_map/ppermute | solution.py:31
  278.6 9.6 %collective-permute-start.13 = (f32[40,1,1024]{2,0,1:T(8,128)S(1)}, f32[40,1,1024]{2,0,1:T(8,128)S(1)}, u32[]{:S(2)}, u32[]{:S(2)}) collective-permute-start(f32[40,1,1024]{2,0,1:T(8,128)S(1)} %get-tuple-element.115), channel_id=1, source_target_pairs={{0,2},{2,4},{4,6},{6,8},{8,10},{10,12},{12,14},{14,16},{16,18},{18... | collective-permute-start | bytes 491528 | tf_op jit(solution)/shard_map/ppermute | solution.py:28
  291.6 15.8 %copy-start.15 = (f32[40,16,1024]{2,0,1:T(8,128)}, f32[40,16,1024]{2,0,1:T(8,128)S(1)}, u32[]{:S(2)}) copy-start(f32[40,16,1024]{2,0,1:T(8,128)S(1)} %get-tuple-element.182) | copy-start | bytes 7864324
  291.6 15.8 %copy-start.16 = (f32[40,16,1024]{2,0,1:T(8,128)}, f32[40,16,1024]{2,0,1:T(8,128)S(1)}, u32[]{:S(2)}) copy-start(f32[40,16,1024]{2,0,1:T(8,128)S(1)} %get-tuple-element.181) | copy-start | bytes 7864324
  291.6 13.7 %collective-permute-start.18 = (f32[40,1,1024]{2,0,1:T(8,128)S(1)}, f32[40,1,1024]{2,0,1:T(8,128)S(1)}, u32[]{:S(2)}, u32[]{:S(2)}) collective-permute-start(f32[40,1,1024]{2,0,1:T(8,128)S(1)} %get-tuple-element.120), channel_id=1, source_target_pairs={{2,0},{4,2},{6,4},{8,6},{10,8},{12,10},{14,12},{16,14},{18,16},{20... | collective-permute-start | bytes 491528 | tf_op jit(solution)/shard_map/ppermute | solution.py:31
  292.9 13.0 %collective-permute-start.19 = (f32[40,1,1024]{2,0,1:T(8,128)S(1)}, f32[40,1,1024]{2,0,1:T(8,128)S(1)}, u32[]{:S(2)}, u32[]{:S(2)}) collective-permute-start(f32[40,1,1024]{2,0,1:T(8,128)S(1)} %get-tuple-element.121), channel_id=1, source_target_pairs={{0,2},{2,4},{4,6},{6,8},{8,10},{10,12},{12,14},{14,16},{16,18},{18... | collective-permute-start | bytes 491528 | tf_op jit(solution)/shard_map/ppermute | solution.py:28
  297.9 18.5 %collective-permute-start.14 = (f32[40,1,1024]{2,0,1:T(8,128)S(1)}, f32[40,1,1024]{2,0,1:T(8,128)}, u32[]{:S(2)}, u32[]{:S(2)}) collective-permute-start(f32[40,1,1024]{2,0,1:T(8,128)S(1)} %get-tuple-element.112), channel_id=1, source_target_pairs={{2,0},{4,2},{6,4},{8,6},{10,8},{12,10},{14,12},{16,14},{18,16},{20... | collective-permute-start | bytes 491528 | tf_op jit(solution)/shard_map/ppermute | solution.py:31
  299.2 17.2 %collective-permute-start.15 = (f32[40,1,1024]{2,0,1:T(8,128)S(1)}, f32[40,1,1024]{2,0,1:T(8,128)}, u32[]{:S(2)}, u32[]{:S(2)}) collective-permute-start(f32[40,1,1024]{2,0,1:T(8,128)S(1)} %get-tuple-element.113), channel_id=1, source_target_pairs={{0,2},{2,4},{4,6},{6,8},{8,10},{10,12},{12,14},{14,16},{16,18},{18... | collective-permute-start | bytes 491528 | tf_op jit(solution)/shard_map/ppermute | solution.py:28
  308.9 7.8 %collective-permute-start.20 = (f32[40,1,1024]{2,0,1:T(8,128)S(1)}, f32[40,1,1024]{2,0,1:T(8,128)}, u32[]{:S(2)}, u32[]{:S(2)}) collective-permute-start(f32[40,1,1024]{2,0,1:T(8,128)S(1)} %get-tuple-element.110), channel_id=1, source_target_pairs={{2,0},{4,2},{6,4},{8,6},{10,8},{12,10},{14,12},{16,14},{18,16},{20... | collective-permute-start | bytes 491528 | tf_op jit(solution)/shard_map/ppermute | solution.py:31
  310.2 7.8 %collective-permute-start.21 = (f32[40,1,1024]{2,0,1:T(8,128)S(1)}, f32[40,1,1024]{2,0,1:T(8,128)}, u32[]{:S(2)}, u32[]{:S(2)}) collective-permute-start(f32[40,1,1024]{2,0,1:T(8,128)S(1)} %get-tuple-element.111), channel_id=1, source_target_pairs={{0,2},{2,4},{4,6},{6,8},{8,10},{10,12},{12,14},{14,16},{16,18},{18... | collective-permute-start | bytes 491528 | tf_op jit(solution)/shard_map/ppermute | solution.py:28
  490.3 7.6 %copy-start.34 = (f32[40,9]{1,0:T(8,128)S(1)}, f32[40,9]{1,0:T(8,128)}, u32[]{:S(2)}) copy-start(f32[40,9]{1,0:T(8,128)} %copy-done.33) | copy-start | bytes 4324
  490.3 10.6 %copy-start.25 = (f32[40,9]{0,1:T(8,128)S(1)}, f32[40,9]{0,1:T(8,128)}, u32[]{:S(2)}) copy-start(f32[40,9]{0,1:T(8,128)} %copy-done.24) | copy-start | bytes 4324
  490.3 16.7 %copy-start.31 = (f32[9,9]{1,0:T(8,128)S(1)}, f32[9,9]{1,0:T(8,128)}, u32[]{:S(2)}) copy-start(f32[9,9]{1,0:T(8,128)} %constant.100.clone) | copy-start | bytes 976
  532.1 24.1 %copy-start.10 = (f32[40,16,1024]{2,0,1:T(8,128)S(1)}, f32[40,16,1024]{2,0,1:T(8,128)}, u32[]{:S(2)}) copy-start(f32[40,16,1024]{2,0,1:T(8,128)} %copy-done.9) | copy-start | bytes 7864324
  532.1 24.1 %copy-start.12 = (f32[40,16,1024]{2,0,1:T(8,128)S(1)}, f32[40,16,1024]{2,0,1:T(8,128)}, u32[]{:S(2)}) copy-start(f32[40,16,1024]{2,0,1:T(8,128)} %copy-done.11) | copy-start | bytes 7864324
  532.1 24.1 %copy-start.14 = (f32[40,16,1024]{2,0,1:T(8,128)S(1)}, f32[40,16,1024]{2,0,1:T(8,128)}, u32[]{:S(2)}) copy-start(f32[40,16,1024]{2,0,1:T(8,128)} %copy-done.13) | copy-start | bytes 7864324
  551.2 5.0 copy-start.5
  551.2 5.0 copy-start.8
  551.2 5.0 copy-start.37
  551.2 5.0 copy-start.48
  551.2 5.0 copy-start.49
  551.3 5.0 copy-start.50
  551.3 5.0 copy-start.51
  551.3 5.0 copy-start.52
  551.3 5.0 copy-start.53
  551.3 5.0 copy-start.54
  556.4 15.6 %copy-start.1 = (bf16[80,136]{0,1:T(8,128)(2,1)S(1)}, bf16[80,136]{0,1:T(8,128)(2,1)}, u32[]{:S(2)}) copy-start(bf16[80,136]{0,1:T(8,128)(2,1)} %param.13) | copy-start | bytes 65284
  (22 other events, 45.7 us)
Sparse Core Ops, SparseCore 0:
  17.1 15.7 reduce-scatter.1
